TPU v7x, 32 devices: a whole 2x2x4 slice. The times are simulated.
32 devices in a mesh: pb: 2 (over x), col: 16 (over z, y, core).
Axes of the slice: x: 2, y: 2, z: 4, core: 2. Of those that a mesh axis runs over, the one named last changes fastest.
Arguments:
- queries: bfloat16 [4096, 1024], P(('pb', 'col')), may hold values from -64 to 64
- candidates: bfloat16 [16384, 1024], P(('col', 'pb')), may hold values from -5 to 5
- grades: int32 [4096, 16384], P('pb', 'col'), may hold values from 0 to 4
- query_weights: float32 [4096], P('pb'), may hold values from -0.046875 to 0.046875
Outputs:
- losses: float32 [4096], P('pb')
- query_grad: bfloat16 [4096, 1024], P(('pb', 'col'))
- cand_grad: bfloat16 [16384, 1024], P(('col', 'pb'))
All inputs are finite; a program needn't handle non-finite values.
Results may differ from a plain program's by a relative error of at most 0.0071.
Values may be sent and summed in bfloat16 or wider, within the bound.
A program may use at most 128 MiB of HBM per device.

v0:
```python
import math
import jax
import jax.numpy as jnp
from jax import lax
from jax.sharding import PartitionSpec as P

GRADES = 5
lowest = -1e30


def combined_all(x, axis, combine):
    everything = jax.tree.map(lambda part: lax.all_gather(part, axis), x)
    leading = jax.tree.map(lambda part: part[0], everything)

    def step(k, so_far):
        return combine(so_far, jax.tree.map(lambda part: part[k], everything))

    return lax.fori_loop(1, lax.axis_size(axis), step, leading)


def grade_levels(maxima, masses, counts):
    levels = []
    running = maxima[0]
    seen_count = counts[0] * 0.0
    for bucket in range(maxima.shape[0]):
        running = jnp.maximum(running, maxima[bucket])
        seen_count = seen_count + counts[bucket]
        summed = masses[0] * jnp.exp(maxima[0] - running)
        for lesser in range(1, bucket + 1):
            summed = summed + masses[lesser] * jnp.exp(maxima[lesser] - running)
        present = seen_count > 0.0
        levels.append(
            jnp.where(present, running + jnp.log(jnp.where(present, summed, 1.0)), running)
        )
    return levels


def slope_factors(maxima, levels, counts):
    factors = []
    for bucket in range(maxima.shape[0]):
        summed = counts[bucket] * jnp.exp(maxima[bucket] - levels[bucket])
        for higher in range(bucket + 1, maxima.shape[0]):
            summed = summed + counts[higher] * jnp.exp(maxima[bucket] - levels[higher])
        factors.append(summed)
    return factors


def local(queries, candidates, grades, query_weights):
    width = queries.shape[1]
    scaling = 1.0 / math.sqrt(width)
    cand_block = lax.all_gather(candidates, "pb", axis=0, tiled=True)
    query_block = lax.all_gather(queries, "col", axis=0, tiled=True)
    scores = jnp.dot(query_block, cand_block.T, preferred_element_type=jnp.float32) * scaling
    members = [grades == bucket for bucket in range(GRADES)]
    totals_local = jnp.sum(scores, axis=1)
    counts_local = jnp.stack([jnp.sum(member.astype(jnp.float32), axis=1) for member in members])
    maxima_local = jnp.stack(
        [jnp.max(jnp.where(member, scores, lowest), axis=1) for member in members]
    )

    def spread_rows(values):
        picked = jnp.zeros(scores.shape, jnp.float32)
        for bucket in range(GRADES):
            picked = jnp.where(members[bucket], values[bucket][:, None], picked)
        return picked

    def masses_from(expo):
        return jnp.stack(
            [jnp.sum(jnp.where(members[bucket], expo, 0.0), axis=1) for bucket in range(GRADES)]
        )

    def combine(former, latter):
        merged = jnp.maximum(former[0], latter[0])
        rescaled = former[1] * jnp.exp(former[0] - merged) + latter[1] * jnp.exp(latter[0] - merged)
        return (merged, rescaled, former[2] + latter[2], former[3] + latter[3])

    expo = jnp.exp(scores - spread_rows(maxima_local))
    maxima, masses, counts, totals = combined_all(
        (maxima_local, masses_from(expo), counts_local, totals_local), "col", combine
    )
    columns_all = grades.shape[1] * lax.axis_size("col")
    levels = grade_levels(maxima, masses, counts)
    weighted = counts[0] * levels[0]
    for bucket in range(1, GRADES):
        weighted = weighted + counts[bucket] * levels[bucket]
    losses = (weighted - totals) / columns_all
    factors = jnp.stack(slope_factors(maxima, levels, counts))
    scaled_factors = factors * jnp.exp(maxima_local - maxima)
    slopes = (query_weights[:, None] * (spread_rows(scaled_factors) * expo - 1.0)).astype(
        jnp.bfloat16
    )
    query_grad = lax.psum_scatter(
        jnp.dot(slopes, cand_block, preferred_element_type=jnp.float32) * scaling,
        "col",
        scatter_dimension=0,
        tiled=True,
    ).astype(jnp.bfloat16)
    cand_grad = lax.psum_scatter(
        lax.dot_general(
            slopes, query_block, (((0,), (0,)), ((), ())), preferred_element_type=jnp.float32
        )
        * scaling,
        "pb",
        scatter_dimension=0,
        tiled=True,
    )
    return (losses, query_grad, cand_grad.astype(jnp.bfloat16))


def solution(mesh):
    in_specs = (P(("pb", "col"), None), P(("col", "pb"), None), P("pb", "col"), P("pb"))
    out_specs = (P("pb"), P(("pb", "col"), None), P(("col", "pb"), None))
    return jax.shard_map(local, mesh=mesh, in_specs=in_specs, out_specs=out_specs, check_vma=False)
```

profile of v0, /device:TPU:0, one launch (start us, length us, event | category | flops | bytes accessed | tf_op | source)
XLA Modules:
  0.0 426.9 jit_solution(16694783811220427614)
XLA Ops:
  7.2 0.7 all-gather.12.cloned.1.call-update
  7.9 0.7 all-gather.10.cloned.1.call-update
  8.7 9.1 %copy.14 = s32[2048,1024]{0,1:T(8,128)} copy(s32[2048,1024]{1,0:T(8,128)} %param.8) | data formatting | bytes 16777216 | tf_op args[2]
  17.8 27.5 %all-gather.12.cloned.1.call-done = bf16[1024,1024]{1,0:T(8,128)(2,1)} async-done(((bf16[512,1024]{1,0:T(8,128)(2,1)}), bf16[1024,1024]{1,0:T(8,128)(2,1)}) %all-gather.12.cloned.1.call-update) | async-done | bytes 2097168 | tf_op jit(solution)/shard_map/all_gather | solution.py:51
  45.4 52.6 %all-gather.10.cloned.1.call-done = bf16[2048,1024]{1,0:T(8,128)(2,1)} async-done(((bf16[128,1024]{1,0:T(8,128)(2,1)}), bf16[2048,1024]{1,0:T(8,128)(2,1)}) %all-gather.10.cloned.1.call-update) | async-done | bytes 4194320 | tf_op jit(solution)/shard_map/all_gather | solution.py:52
  97.9 19.5 %multiply_reduce_fusion = (f32[2048]{0:T(1024)S(1)}, f32[2048]{0:T(1024)S(1)}, f32[2048]{0:T(1024)S(1)}, f32[2048]{0:T(1024)S(1)}, f32[2048]{0:T(1024)S(1)}, /*i...) fusion(s32[2048,1024]{0,1:T(8,128)} %copy.14, ...), kind=kOutput, calls=%fused_computation.24 | convolution fusion | flops 4334798848 | bytes 33611776 | tf_op jit(solution)/shard_map/dot_general | solution.py:53
  117.5 19.3 %all-gather.3 = f32[32768]{0:T(1024)S(1)} all-gather(f32[2048]{0:T(1024)S(1)} %get-tuple-element.236), channel_id=5, replica_groups=mesh['pb'=2,'col'=16] {'col'}, dimensions={0}, use_global_device_ids=true | all-gather | bytes 139264 | tf_op jit(solution)/shard_map/all_gather | solution.py:12
  136.8 16.7 %select_reduce_fusion = (f32[2048]{0:T(1024)S(1)}, f32[2048]{0:T(1024)S(1)}, f32[2048]{0:T(1024)S(1)}, f32[2048]{0:T(1024)S(1)}, f32[2048]{0:T(1024)}, /*index=5...) fusion(pred[2048,1024]{0,1:T(8,128)(4,1)} %get-tuple-element.282, ...), kind=kLoop, calls=%fused_computation.13 | loop fusion | flops 52410368 | bytes 27377664 | tf_op jit(solution)/shard_map/reduce_sum | solution.py:69
  153.5 0.1 stack.79
  153.6 20.8 %all-gather.6 = f32[16,5,2048]{2,1,0:T(8,128)S(1)} all-gather(f32[1,5,2048]{2,1,0:T(8,128)S(1)} %bitcast.71), channel_id=4, replica_groups=mesh['pb'=2,'col'=16] {'col'}, dimensions={0}, use_global_device_ids=true | all-gather | bytes 696320 | tf_op jit(solution)/shard_map/all_gather | solution.py:12
  174.4 0.8 stack.73
  175.2 25.6 %all-gather.5 = f32[16,5,2048]{2,1,0:T(8,128)S(1)} all-gather(f32[1,5,2048]{2,1,0:T(8,128)S(1)} %bitcast.72), channel_id=3, replica_groups=mesh['pb'=2,'col'=16] {'col'}, dimensions={0}, use_global_device_ids=true | all-gather | bytes 696320 | tf_op jit(solution)/shard_map/all_gather | solution.py:12
  200.8 1.1 copy-done.1
  201.8 0.8 stack.67
  202.6 20.7 %all-gather.4 = f32[16,5,2048]{2,1,0:T(8,128)S(1)} all-gather(f32[1,5,2048]{2,1,0:T(8,128)S(1)} %bitcast.70), channel_id=2, replica_groups=mesh['pb'=2,'col'=16] {'col'}, dimensions={0}, use_global_device_ids=true | all-gather | bytes 696320 | tf_op jit(solution)/shard_map/all_gather | solution.py:12
  223.3 1.0 copy-done.2
  224.3 15.0 %while.21 = (s32[]{:T(128)}, f32[5,2048]{1,0:T(8,128)S(1)}, f32[5,2048]{1,0:T(8,128)S(1)}, f32[5,2048]{1,0:T(8,128)S(1)}, f32[2048]{0:T(1024)S(1)}, /*index=5*/f...) while((s32[]{:T(128)}, f32[5,2048]{1,0:T(8,128)S(1)}, ...), condition=%wide.region_17.18_spmd, body=%wide.region_16.17_spmd.sunk | while | flops 73733 | bytes 409767 | solution.py:18
  224.3 0.9 fusion.46
  225.3 0.9 fusion.46
  226.3 0.9 fusion.46
  227.3 0.9 fusion.46
  228.3 0.9 fusion.46
  229.3 0.9 fusion.46
  230.3 0.9 fusion.46
  231.3 0.9 fusion.46
  232.3 0.9 fusion.46
  233.3 0.9 fusion.46
  234.3 0.9 fusion.46
  235.3 0.9 fusion.46
  236.3 0.9 fusion.46
  237.3 0.9 fusion.46
  238.3 0.9 fusion.46
  239.3 0.2 exponential_multiply_fusion.1
  239.5 0.2 multiply_add_fusion.2
  239.7 0.1 multiply_add_fusion.3
  239.8 0.1 multiply_add_fusion.4
  239.9 0.2 multiply_add_fusion.5
  240.1 0.1 stack.80
  240.2 8.7 %multiply_convert_fusion = bf16[2048,1024]{0,1:T(8,128)(2,1)S(1)} fusion(f32[2048,1024]{0,1:T(8,128)} %get-tuple-element.280, pred[2048,1024]{0,1:T(8,128)(4,1)} %get-tuple-element.282, pred[2048,1024]{0,1:T(8,128)(4,1)} %get-tuple-element.283, pred[2048,1024]{0,1:T(8,128)(4,1)} %get-tuple-element.284, pred[2048,1024]{0,1:T(8,128)(4,1)} %get-tuple-element.285, ...), kind=kLoop, calls=%fused_computation.7 | loop fusion | flops 18874368 | bytes 23117824 | tf_op jit(solution)/shard_map/convert_element_type | solution.py:89
  249.0 2.0 copy-done
  250.9 6.0 %convolution_multiply_fusion.1 = f32[1024,1024]{1,0:T(8,128)} fusion(bf16[2048,1024]{0,1:T(8,128)(2,1)S(1)} %multiply_convert_fusion, bf16[2048,1024]{1,0:T(8,128)(2,1)S(1)} %copy-done.7), kind=kOutput, calls=%fused_computation.31 | convolution fusion | flops 4296015872 | bytes 12582912 | tf_op jit(solution)/shard_map/dot_general | solution.py:99
  257.0 9.0 %convolution_multiply_fusion = f32[2048,1024]{0,1:T(8,128)} fusion(bf16[2048,1024]{0,1:T(8,128)(2,1)} %copy-done, bf16[1024,1024]{1,0:T(8,128)(2,1)S(1)} %copy-done.8), kind=kOutput, calls=%fused_computation.25 | convolution fusion | flops 4297064448 | bytes 14680064 | tf_op jit(solution)/shard_map/dot_general | solution.py:93
  266.1 0.7 fusion.9
  266.7 44.2 %reduce-scatter.5.cloned.1.call-done = f32[512,1024]{1,0:T(8,128)} async-done(((f32[1024,1024]{1,0:T(8,128)}), f32[512,1024]{1,0:T(8,128)}) %reduce-scatter.5.cloned.1.call-update) | async-done | bytes 2097168 | tf_op jit(solution)/shard_map/reduce_scatter | solution.py:98
  310.9 2.7 convert_element_type.31
  313.7 104.8 %reduce-scatter.3.cloned.1.call-done = f32[128,1024]{0,1:T(8,128)} async-done(((f32[2048,1024]{0,1:T(8,128)}), f32[128,1024]{0,1:T(8,128)}) %reduce-scatter.3.cloned.1.call-update) | async-done | bytes 524304 | tf_op jit(solution)/shard_map/reduce_scatter | solution.py:92
  418.5 1.1 convert_element_type.30
  419.5 0.8 copy.20
  (58 shorter events, 0.6 us)
Async XLA Ops:
  7.2 38.2 %all-gather.12.cloned.1.call-start = ((), (), s32[]{:S(2)}) async-start(), calls=%async_computation.3 | async-start | bytes 3145728 | tf_op jit(solution)/shard_map/all_gather | solution.py:51
  7.9 90.0 %all-gather.10.cloned.1.call-start = ((), (), s32[]{:S(2)}) async-start(), calls=%async_computation.2 | async-start | bytes 4456448 | tf_op jit(solution)/shard_map/all_gather | solution.py:52
  8.6 302.3 %reduce-scatter.5.cloned.1.call-start = ((), (), s32[]{:S(2)}) async-start(), calls=%async_computation.5 | async-start | bytes 6291456 | tf_op jit(solution)/shard_map/reduce_scatter | solution.py:98
  117.5 36.0 %copy-start.3 = (f32[2048]{0:T(1024)}, f32[2048]{0:T(1024)S(1)}, u32[]{:S(2)}) copy-start(f32[2048]{0:T(1024)S(1)} %get-tuple-element.238) | copy-start | bytes 24580
  117.5 36.0 %copy-start.4 = (f32[2048]{0:T(1024)}, f32[2048]{0:T(1024)S(1)}, u32[]{:S(2)}) copy-start(f32[2048]{0:T(1024)S(1)} %get-tuple-element.239) | copy-start | bytes 24580
  117.5 36.0 %copy-start.5 = (f32[2048]{0:T(1024)}, f32[2048]{0:T(1024)S(1)}, u32[]{:S(2)}) copy-start(f32[2048]{0:T(1024)S(1)} %get-tuple-element.240) | copy-start | bytes 24580
  117.5 36.0 %copy-start.6 = (f32[2048]{0:T(1024)}, f32[2048]{0:T(1024)S(1)}, u32[]{:S(2)}) copy-start(f32[2048]{0:T(1024)S(1)} %get-tuple-element.241) | copy-start | bytes 24580
  200.8 1.1 copy-start.1
  223.3 1.0 copy-start.2
  240.2 10.7 %copy-start.7 = (bf16[2048,1024]{1,0:T(8,128)(2,1)S(1)}, bf16[2048,1024]{1,0:T(8,128)(2,1)}, u32[]{:S(2)}) copy-start(bf16[2048,1024]{1,0:T(8,128)(2,1)} %all-gather.10.cloned.1.call-done) | copy-start | bytes 12582916
  249.0 2.0 copy-start
  250.9 6.1 %copy-start.8 = (bf16[1024,1024]{1,0:T(8,128)(2,1)S(1)}, bf16[1024,1024]{1,0:T(8,128)(2,1)}, u32[]{:S(2)}) copy-start(bf16[1024,1024]{1,0:T(8,128)(2,1)} %all-gather.12.cloned.1.call-done) | copy-start | bytes 6291460
  257.0 161.5 %reduce-scatter.3.cloned.1.call-start = ((), (), s32[]{:S(2)}) async-start(), calls=%async_computation.4 | async-start | bytes 8912896 | tf_op jit(solution)/shard_map/reduce_scatter | solution.py:92
Sparse Core Ops, SparseCore 0:
  9.5 35.8 all-gather.11
  47.5 50.3 all-gather.9
  257.1 53.7 reduce-scatter.4
  314.9 103.5 reduce-scatter.2
where the time goes:
time: 428 us; the launch traced here: 427 us
  waiting for transfers between devices  231 us (54%)
  blocking collectives  86.4 us (20%)
  other arithmetic  44.8 us (10%)
  matrix products  34.6 us (8%)
  local copies, waits for them, and re-layouts  16 us (4%)
  between operations  13.9 us (3%)
    reduce_scatter x1, waiting for transfers between devices, local(): lax.psum_scatter(jnp.dot(slopes, cand_block, preferred_element_type=jnp.f...  105 us
    all_gather x4, blocking collectives, combined_all(): everything = jax.tree.map(lambda part: lax.all_gather(part, axis), x)  86.4 us
    all_gather x1, waiting for transfers between devices, local(): query_block = lax.all_gather(queries, 'col', axis=0, tiled=True)  52.6 us
    reduce_scatter x1, waiting for transfers between devices, local(): lax.psum_scatter(lax.dot_general(slopes, query_block, (((0,), (0,)), ((),...  44.2 us
    all_gather x1, waiting for transfers between devices, local(): cand_block = lax.all_gather(candidates, 'pb', axis=0, tiled=True)  27.5 us
    dot_general x1, matrix products, local(): jnp.dot(query_block, cand_block.T, preferred_element_type=jnp.float32)  19.5 us
    reduce_sum x1, other arithmetic, masses_from(): jnp.sum(jnp.where(members[bucket], expo, 0.0), axis=1)  16.7 us
    add x15, other arithmetic, combine(): former[1] * jnp.exp(former[0] - merged)  14.2 us
  transfers between devices with their start and end apart: 4, of which 4 were waited for; matrix products, arithmetic and copies ran while one was open for 5% of the time, Pallas kernels for 0%

commit v1 on v0

--- a/solution.py
+++ b/solution.py
@@ -49,7 +49,9 @@
     width = queries.shape[1]
     scaling = 1.0 / math.sqrt(width)
     cand_block = lax.all_gather(candidates, "pb", axis=0, tiled=True)
-    query_block = lax.all_gather(queries, "col", axis=0, tiled=True)
+    query_block = jnp.concatenate(
+        lax.all_to_all(jnp.stack([queries] * lax.axis_size("col")), "col", 0, 0), axis=0
+    )
     scores = jnp.dot(query_block, cand_block.T, preferred_element_type=jnp.float32) * scaling
     members = [grades == bucket for bucket in range(GRADES)]
     totals_local = jnp.sum(scores, axis=1)

time: 428 us -> 442 us (1.033)
  blocking collectives: 86.4 us -> 101 us
  waiting for transfers between devices: 231 us -> 217 us
  starting transfers between devices: 0.16 us -> 7.59 us
    all_gather x1 -> x0, waiting for transfers between devices: 52.6 us -> none  [local(): query_block = lax.all_gather(queries, 'col', axis=0, tiled=True)]
    all_to_all x0 -> x1, waiting for transfers between devices: none -> 40.8 us  [local(): lax.all_to_all(jnp.stack([queries] * lax.axis_size('col')), 'col', 0, 0)]
    all_gather x4, blocking collectives: 86.4 us -> 101 us  [combined_all(): everything = jax.tree.map(lambda part: lax.all_gather(part, axis), x)]
    all_to_all x0 -> x1, starting transfers between devices: none -> 7.46 us  [local(): lax.all_to_all(jnp.stack([queries] * lax.axis_size('col')), 'col', 0, 0)]
    unnamed x20 -> x18, local copies, waits for them, and re-layouts: 14 us -> 14 us
where the time goes in v1:
time: 442 us; the launch traced here: 441 us
  waiting for transfers between devices  217 us (49%)
  blocking collectives  101 us (23%)
  other arithmetic  44.7 us (10%)
  matrix products  36.9 us (8%)
  local copies, waits for them, and re-layouts  19.4 us (4%)
  between operations  13.9 us (3%)
  starting transfers between devices  7.59 us (2%)
    reduce_scatter x1, waiting for transfers between devices, local(): lax.psum_scatter(jnp.dot(slopes, cand_block, preferred_element_type=jnp.f...  105 us
    all_gather x4, blocking collectives, combined_all(): everything = jax.tree.map(lambda part: lax.all_gather(part, axis), x)  101 us
    reduce_scatter x1, waiting for transfers between devices, local(): lax.psum_scatter(lax.dot_general(slopes, query_block, (((0,), (0,)), ((),...  43.7 us
    all_to_all x1, waiting for transfers between devices, local(): lax.all_to_all(jnp.stack([queries] * lax.axis_size('col')), 'col', 0, 0)  40.8 us
    all_gather x1, waiting for transfers between devices, local(): cand_block = lax.all_gather(candidates, 'pb', axis=0, tiled=True)  26.8 us
    dot_general x1, matrix products, local(): jnp.dot(query_block, cand_block.T, preferred_element_type=jnp.float32)  19.5 us
    reduce_sum x1, other arithmetic, masses_from(): jnp.sum(jnp.where(members[bucket], expo, 0.0), axis=1)  16.7 us
    add x15, other arithmetic, combine(): former[1] * jnp.exp(former[0] - merged)  14.2 us
  transfers between devices with their start and end apart: 4, of which 4 were waited for; matrix products, arithmetic and copies ran while one was open for 5% of the time, Pallas kernels for 0%

profile of v1, /device:TPU:0, one launch (start us, length us, event | category | flops | bytes accessed | tf_op | source)
XLA Modules:
  0.0 440.8 jit_solution(4253275862876253926)
XLA Ops:
  7.2 3.4 stack.40
  10.6 7.5 %all-to-all-start = ((bf16[16,128,1024]{2,1,0:T(8,128)(2,1)}), bf16[16,128,1024]{2,1,0:T(8,128)(2,1)}, u32[]{:S(2)}, u32[]{:S(2)}) async-start(bf16[16,128,1024]{2,1,0:T(8,128)(2,1)} %stack.40), calls=%async_computation | async-start | bytes 8388608 | tf_op jit(solution)/shard_map/all_to_all | solution.py:53
  18.1 0.7 all-gather.9.cloned.1.call-update
  18.8 9.1 %copy.14 = s32[2048,1024]{0,1:T(8,128)} copy(s32[2048,1024]{1,0:T(8,128)} %param.8) | data formatting | bytes 16777216 | tf_op args[2]
  28.0 26.8 %all-gather.9.cloned.1.call-done = bf16[1024,1024]{1,0:T(8,128)(2,1)} async-done(((bf16[512,1024]{1,0:T(8,128)(2,1)}), bf16[1024,1024]{1,0:T(8,128)(2,1)}) %all-gather.9.cloned.1.call-update) | async-done | bytes 2097168 | tf_op jit(solution)/shard_map/all_gather | solution.py:51
  54.8 40.8 %all-to-all-done = bf16[16,128,1024]{2,1,0:T(8,128)(2,1)} async-done(((bf16[16,128,1024]{2,1,0:T(8,128)(2,1)}), bf16[16,128,1024]{2,1,0:T(8,128)(2,1)}, u32[]{:S(2)}, u32[]{:S(2)}) %all-to-all-start) | async-done | bytes 4194336 | tf_op jit(solution)/shard_map/all_to_all | solution.py:53
  95.6 19.5 %multiply_reduce_fusion = (f32[2048]{0:T(1024)S(1)}, f32[2048]{0:T(1024)S(1)}, f32[2048]{0:T(1024)S(1)}, f32[2048]{0:T(1024)S(1)}, f32[2048]{0:T(1024)S(1)}, /*i...) fusion(s32[2048,1024]{0,1:T(8,128)} %copy.14, ...), kind=kOutput, calls=%fused_computation.24 | convolution fusion | flops 4334798848 | bytes 33611776 | tf_op jit(solution)/shard_map/dot_general | solution.py:55
  115.2 35.7 %all-gather.3 = f32[32768]{0:T(1024)S(1)} all-gather(f32[2048]{0:T(1024)S(1)} %get-tuple-element.236), channel_id=5, replica_groups=mesh['pb'=2,'col'=16] {'col'}, dimensions={0}, use_global_device_ids=true | all-gather | bytes 139264 | tf_op jit(solution)/shard_map/all_gather | solution.py:12
  150.9 16.7 %select_reduce_fusion = (f32[2048]{0:T(1024)S(1)}, f32[2048]{0:T(1024)S(1)}, f32[2048]{0:T(1024)S(1)}, f32[2048]{0:T(1024)S(1)}, f32[2048]{0:T(1024)}, /*index=5...) fusion(pred[2048,1024]{0,1:T(8,128)(4,1)} %get-tuple-element.282, ...), kind=kLoop, calls=%fused_computation.13 | loop fusion | flops 52410368 | bytes 27377664 | tf_op jit(solution)/shard_map/reduce_sum | solution.py:71
  167.6 20.5 %all-gather.6 = f32[16,5,2048]{2,1,0:T(8,128)S(1)} all-gather(f32[1,5,2048]{2,1,0:T(8,128)S(1)} %bitcast.72), channel_id=4, replica_groups=mesh['pb'=2,'col'=16] {'col'}, dimensions={0}, use_global_device_ids=true | all-gather | bytes 696320 | tf_op jit(solution)/shard_map/all_gather | solution.py:12
  188.1 0.8 stack.93
  188.9 23.7 %all-gather.5 = f32[16,5,2048]{2,1,0:T(8,128)S(1)} all-gather(f32[1,5,2048]{2,1,0:T(8,128)S(1)} %bitcast.73), channel_id=3, replica_groups=mesh['pb'=2,'col'=16] {'col'}, dimensions={0}, use_global_device_ids=true | all-gather | bytes 696320 | tf_op jit(solution)/shard_map/all_gather | solution.py:12
  212.6 1.1 copy-done.1
  213.7 0.8 stack.87
  214.5 20.8 %all-gather.4 = f32[16,5,2048]{2,1,0:T(8,128)S(1)} all-gather(f32[1,5,2048]{2,1,0:T(8,128)S(1)} %bitcast.71), channel_id=2, replica_groups=mesh['pb'=2,'col'=16] {'col'}, dimensions={0}, use_global_device_ids=true | all-gather | bytes 696320 | tf_op jit(solution)/shard_map/all_gather | solution.py:12
  235.3 1.0 copy-done.2
  236.3 15.0 %while.21 = (s32[]{:T(128)}, f32[5,2048]{1,0:T(8,128)S(1)}, f32[5,2048]{1,0:T(8,128)S(1)}, f32[5,2048]{1,0:T(8,128)S(1)}, f32[2048]{0:T(1024)S(1)}, /*index=5*/f...) while((s32[]{:T(128)}, f32[5,2048]{1,0:T(8,128)S(1)}, ...), condition=%wide.region_17.18_spmd, body=%wide.region_16.17_spmd.sunk | while | flops 73733 | bytes 409767 | solution.py:18
  236.3 0.9 fusion.46
  237.3 0.9 fusion.46
  238.3 0.9 fusion.46
  239.3 0.9 fusion.46
  240.3 0.9 fusion.46
  241.3 0.9 fusion.46
  242.3 0.9 fusion.46
  243.3 0.9 fusion.46
  244.3 0.9 fusion.46
  245.3 0.9 fusion.46
  246.3 0.9 fusion.46
  247.3 0.9 fusion.46
  248.3 0.9 fusion.46
  249.3 0.9 fusion.46
  250.3 0.9 fusion.46
  251.3 0.2 exponential_multiply_fusion.1
  251.5 0.2 multiply_add_fusion.2
  251.7 0.1 multiply_add_fusion.3
  251.8 0.1 multiply_add_fusion.4
  251.9 0.2 multiply_add_fusion.5
  252.1 0.1 stack.100
  252.2 8.6 %multiply_convert_fusion = bf16[2048,1024]{0,1:T(8,128)(2,1)S(1)} fusion(f32[2048,1024]{0,1:T(8,128)} %get-tuple-element.280, pred[2048,1024]{0,1:T(8,128)(4,1)} %get-tuple-element.282, pred[2048,1024]{0,1:T(8,128)(4,1)} %get-tuple-element.283, pred[2048,1024]{0,1:T(8,128)(4,1)} %get-tuple-element.284, pred[2048,1024]{0,1:T(8,128)(4,1)} %get-tuple-element.285, ...), kind=kLoop, calls=%fused_computation.7 | loop fusion | flops 18874368 | bytes 23117824 | tf_op jit(solution)/shard_map/convert_element_type | solution.py:91
  260.8 1.9 copy-done
  262.8 8.4 %convolution_multiply_fusion.1 = f32[1024,1024]{1,0:T(8,128)} fusion(bf16[2048,1024]{0,1:T(8,128)(2,1)S(1)} %multiply_convert_fusion, bf16[2048,1024]{1,0:T(8,128)(2,1)} %bitcast.4), kind=kOutput, calls=%fused_computation.31 | convolution fusion | flops 4296015872 | bytes 12582912 | tf_op jit(solution)/shard_map/dot_general | solution.py:101
  271.2 9.0 %convolution_multiply_fusion = f32[2048,1024]{0,1:T(8,128)} fusion(bf16[2048,1024]{0,1:T(8,128)(2,1)} %copy-done, bf16[1024,1024]{1,0:T(8,128)(2,1)S(1)} %copy-done.7), kind=kOutput, calls=%fused_computation.25 | convolution fusion | flops 4297064448 | bytes 14680064 | tf_op jit(solution)/shard_map/dot_general | solution.py:95
  280.3 0.7 fusion.9
  280.9 43.7 %reduce-scatter.5.cloned.1.call-done = f32[512,1024]{1,0:T(8,128)} async-done(((f32[1024,1024]{1,0:T(8,128)}), f32[512,1024]{1,0:T(8,128)}) %reduce-scatter.5.cloned.1.call-update) | async-done | bytes 2097168 | tf_op jit(solution)/shard_map/reduce_scatter | solution.py:100
  324.6 2.7 convert_element_type.31
  327.3 105.0 %reduce-scatter.3.cloned.1.call-done = f32[128,1024]{0,1:T(8,128)} async-done(((f32[2048,1024]{0,1:T(8,128)}), f32[128,1024]{0,1:T(8,128)}) %reduce-scatter.3.cloned.1.call-update) | async-done | bytes 524304 | tf_op jit(solution)/shard_map/reduce_scatter | solution.py:94
  432.3 1.1 convert_element_type.30
  433.4 0.8 copy.20
  (56 shorter events, 0.7 us)
Async XLA Ops:
  10.6 85.0 %all-to-all-start = ((bf16[16,128,1024]{2,1,0:T(8,128)(2,1)}), bf16[16,128,1024]{2,1,0:T(8,128)(2,1)}, u32[]{:S(2)}, u32[]{:S(2)}) async-start(bf16[16,128,1024]{2,1,0:T(8,128)(2,1)} %stack.40), calls=%async_computation | async-start | bytes 8388608 | tf_op jit(solution)/shard_map/all_to_all | solution.py:53
  18.0 36.7 %all-gather.9.cloned.1.call-start = ((), (), s32[]{:S(2)}) async-start(), calls=%async_computation.3 | async-start | bytes 3145728 | tf_op jit(solution)/shard_map/all_gather | solution.py:51
  18.8 305.8 %reduce-scatter.5.cloned.1.call-start = ((), (), s32[]{:S(2)}) async-start(), calls=%async_computation.5 | async-start | bytes 6291456 | tf_op jit(solution)/shard_map/reduce_scatter | solution.py:100
  115.1 52.4 %copy-start.3 = (f32[2048]{0:T(1024)}, f32[2048]{0:T(1024)S(1)}, u32[]{:S(2)}) copy-start(f32[2048]{0:T(1024)S(1)} %get-tuple-element.238) | copy-start | bytes 24580
  115.1 52.4 %copy-start.4 = (f32[2048]{0:T(1024)}, f32[2048]{0:T(1024)S(1)}, u32[]{:S(2)}) copy-start(f32[2048]{0:T(1024)S(1)} %get-tuple-element.239) | copy-start | bytes 24580
  115.1 52.4 %copy-start.5 = (f32[2048]{0:T(1024)}, f32[2048]{0:T(1024)S(1)}, u32[]{:S(2)}) copy-start(f32[2048]{0:T(1024)S(1)} %get-tuple-element.240) | copy-start | bytes 24580
  115.1 52.4 %copy-start.6 = (f32[2048]{0:T(1024)}, f32[2048]{0:T(1024)S(1)}, u32[]{:S(2)}) copy-start(f32[2048]{0:T(1024)S(1)} %get-tuple-element.241) | copy-start | bytes 24580
  212.6 1.1 copy-start.1
  235.3 1.0 copy-start.2
  260.8 2.0 copy-start
  262.8 8.5 %copy-start.7 = (bf16[1024,1024]{1,0:T(8,128)(2,1)S(1)}, bf16[1024,1024]{1,0:T(8,128)(2,1)}, u32[]{:S(2)}) copy-start(bf16[1024,1024]{1,0:T(8,128)(2,1)} %all-gather.9.cloned.1.call-done) | copy-start | bytes 6291460
  271.2 161.1 %reduce-scatter.3.cloned.1.call-start = ((), (), s32[]{:S(2)}) async-start(), calls=%async_computation.4 | async-start | bytes 8912896 | tf_op jit(solution)/shard_map/reduce_scatter | solution.py:94
Sparse Core Ops, SparseCore 0:
  20.4 34.3 all-gather.8
  271.3 53.2 reduce-scatter.4
  328.7 103.5 reduce-scatter.2
